TPU v7x, 64 devices: a 2x2x8 block of a 4x4x8 slice. The times are simulated.
64 devices in a mesh: dp: 4 (over x, y), tp: 16 (over z, core).
Axes of the slice: x: 2, y: 2, z: 8, core: 2. Of those that a mesh axis runs over, the one named last changes fastest.
The devices are a block of a 4x4x8 slice.
Arguments:
- x: bfloat16 [512, 2048], P('dp'), parts along dimension 0
- lengths: int32 [512], P('dp'), parts along dimension 0
- k_cache: bfloat16 [2, 512, 128, 16, 128], P(None, 'dp', None, 'tp'), parts along dimension 1
- v_cache: bfloat16 [2, 512, 128, 16, 128], P(None, 'dp', None, 'tp'), parts along dimension 1
- attn_norm: float32 [2, 2048], replicated
- mlp_norm: float32 [2, 2048], replicated
- w_q: bfloat16 [2, 2048, 2048], P(None, None, 'tp')
- w_k: bfloat16 [2, 2048, 2048], P(None, None, 'tp')
- w_v: bfloat16 [2, 2048, 2048], P(None, None, 'tp')
- w_o: bfloat16 [2, 2048, 2048], P(None, 'tp')
- w_gate: bfloat16 [2, 2048, 8192], P(None, None, 'tp')
- w_up: bfloat16 [2, 2048, 8192], P(None, None, 'tp')
- w_down: bfloat16 [2, 8192, 2048], P(None, 'tp')
Outputs:
- output: bfloat16 [512, 2048], P('dp'), parts along dimension 0
There are 4 independent parts. A program takes and returns all parts, laid end to end along the dimension named above; an argument that names none is the same for every part.
All inputs are finite; a program needn't handle non-finite values.
Results may differ from a plain program's by a relative error of at most 0.02.
Values are sent between devices in bfloat16 or wider.
A program may use at most 768 MiB of HBM per device.

v0:
```python
import jax
import jax.numpy as jnp
from jax import lax
from jax.sharding import PartitionSpec as P

NORM_EPS = 1e-5
ROPE_BASE = 10000.0


def rms_norm(hidden_in, norm_gain):
    mean_sq = jnp.mean(hidden_in * hidden_in, axis=-1, keepdims=True)
    return (hidden_in * lax.rsqrt(mean_sq + NORM_EPS) * norm_gain).astype(jnp.bfloat16)


def rope_tables(lengths, head_dim):
    inv_freq = ROPE_BASE ** (-jnp.arange(0, head_dim, 2).astype(jnp.float32) / head_dim)
    angles = lengths.astype(jnp.float32)[:, None] * inv_freq[None, :]
    return jnp.cos(angles)[:, None, :], jnp.sin(angles)[:, None, :]


def apply_rope(proj_out, cos_t, sin_t):
    half_dim = proj_out.shape[-1] // 2
    first_half = proj_out[..., :half_dim]
    second_half = proj_out[..., half_dim:]
    return jnp.concatenate([first_half * cos_t - second_half * sin_t, second_half * cos_t + first_half * sin_t], axis=-1)


def attention(q_heads, k_new, v_new, k_layer, v_layer, lengths):
    batch_n, seq_n, kv_heads, head_dim = k_layer.shape
    group_n = q_heads.shape[1] // kv_heads
    inv_scale = head_dim ** -0.5
    q_group = q_heads.reshape(batch_n, kv_heads, group_n, head_dim)
    logits = jnp.einsum("bkgd,bskd->bkgs", q_group, k_layer, preferred_element_type=jnp.float32) * inv_scale
    valid_mask = jnp.arange(seq_n)[None, None, None, :] < lengths[:, None, None, None]
    logits = jnp.where(valid_mask, logits, -1e30)
    logit_new = jnp.einsum("clhe,cle->clh", q_group, k_new, preferred_element_type=jnp.float32) * inv_scale
    row_max = jnp.maximum(jnp.max(logits, axis=-1), logit_new)
    prob_cache = jnp.exp(logits - row_max[..., None])
    prob_new = jnp.exp(logit_new - row_max)
    prob_sum = jnp.sum(prob_cache, axis=-1) + prob_new
    weighted = jnp.einsum("bkgs,bskd->bkgd", prob_cache.astype(jnp.bfloat16), v_layer, preferred_element_type=jnp.float32)
    weighted = weighted + prob_new.astype(jnp.bfloat16).astype(jnp.float32)[..., None] * v_new.astype(jnp.float32)[:, :, None, :]
    return (weighted / prob_sum[..., None]).astype(jnp.bfloat16).reshape(batch_n, -1)


def solution(mesh):
    tp_size = mesh.shape["tp"]
    cache_spec = P(None, "dp", None, "tp", None)
    col_spec = P(None, None, "tp")
    row_spec = P(None, "tp", None)
    in_specs = (P("dp", None), P("dp"), cache_spec, cache_spec, P(), P(), col_spec, col_spec, col_spec, row_spec, col_spec, col_spec, row_spec)

    def reduce_add(activations, weight, resid_f):
        weight_blocks = weight.reshape(weight.shape[0], tp_size, -1)
        partials = jnp.einsum("bk,ktn->tbn", activations, weight_blocks, preferred_element_type=jnp.float32).astype(jnp.bfloat16)
        received = lax.all_to_all(partials, "tp", 0, 0, tiled=True)
        col_width = resid_f.shape[1] // tp_size
        own_cols = lax.dynamic_slice_in_dim(resid_f, lax.axis_index("tp") * col_width, col_width, axis=1)
        new_cols = (own_cols + jnp.sum(received.astype(jnp.float32), axis=0)).astype(jnp.bfloat16)
        return lax.all_gather(new_cols, "tp", axis=1, tiled=True)

    def local_layers(x, lengths, k_cache, v_cache, attn_norm, mlp_norm, w_q, w_k, w_v, w_o, w_gate, w_up, w_down):
        batch_n = x.shape[0]
        head_dim = k_cache.shape[4]
        kv_heads = k_cache.shape[3]
        heads_loc = w_q.shape[2] // head_dim
        cos_t, sin_t = rope_tables(lengths, head_dim)
        residual = x
        for layer_idx in range(w_q.shape[0]):
            resid_f = residual.astype(jnp.float32)
            normed = rms_norm(resid_f, attn_norm[layer_idx])
            q_proj = jnp.dot(normed, w_q[layer_idx], preferred_element_type=jnp.float32)
            k_proj = jnp.dot(normed, w_k[layer_idx], preferred_element_type=jnp.float32)
            q_heads = apply_rope(q_proj.reshape(batch_n, heads_loc, head_dim), cos_t, sin_t).astype(jnp.bfloat16)
            k_new = apply_rope(k_proj.reshape(batch_n, kv_heads, head_dim), cos_t, sin_t).astype(jnp.bfloat16)
            v_new = jnp.dot(normed, w_v[layer_idx], preferred_element_type=jnp.float32).astype(jnp.bfloat16).reshape(batch_n, kv_heads, head_dim)
            attn_out = attention(q_heads, k_new, v_new, k_cache[layer_idx], v_cache[layer_idx], lengths)
            hidden_f = reduce_add(attn_out, w_o[layer_idx], resid_f).astype(jnp.float32)
            normed_mlp = rms_norm(hidden_f, mlp_norm[layer_idx])
            gate_proj = jnp.dot(normed_mlp, w_gate[layer_idx], preferred_element_type=jnp.float32)
            up_proj = jnp.dot(normed_mlp, w_up[layer_idx], preferred_element_type=jnp.float32)
            mlp_act = (jax.nn.silu(gate_proj) * up_proj).astype(jnp.bfloat16)
            residual = reduce_add(mlp_act, w_down[layer_idx], hidden_f)
        return residual

    return jax.shard_map(local_layers, mesh=mesh, in_specs=in_specs, out_specs=P("dp", None), check_vma=False)
```

profile of v0, /device:TPU:21, one launch (start us, length us, event | category | flops | bytes accessed | tf_op | source)
XLA Modules:
  0.0 205.6 jit_solution(7780456938190431005)
XLA Ops:
  0.0 2.2 %fusion.153 = (bf16[1,128,2048]{2,1,0:T(8,128)(2,1)S(1)}, bf16[1,128,2048]{2,1,0:T(8,128)(2,1)}) fusion(bf16[2,128,2048]{2,1,0:T(8,128)(2,1)} %param.22), kind=kLoop, calls=%fused_computation.181 | loop fusion | bytes 2097152 | tf_op jit(solution)/shard_map/slice | solution.py:78
  7.6 4.5 %fusion.6 = f32[128,1,128]{2,1,0:T(1,128)S(1)} fusion(bf16[128,128,1]{1,2,0:T(2,128)(2,1)S(1)} %copy.30, bf16[2,128,128,1,128]{4,2,3,1,0:T(8,128)(2,1)} %param.15), kind=kOutput, calls=%fused_computation.6 | convolution fusion | flops 4194304 | bytes 4292608 | tf_op jit(solution)/shard_map/bkgd,bskd->bkgs/dot_general | solution.py:33
  12.6 3.4 %fusion.4 = f32[128,1,128]{2,1,0:T(1,128)S(1)} fusion(bf16[2,128,128,1,128]{4,2,3,1,0:T(8,128)(2,1)} %param.16, bf16[128,128,1]{1,0,2:T(8,128)(2,1)S(1)} %get-tuple-element.16), kind=kOutput, calls=%fused_computation.4 | convolution fusion | flops 4194304 | bytes 4292608 | tf_op jit(solution)/shard_map/bkgs,bskd->bkgd/dot_general | solution.py:41
  17.4 10.7 %all-to-all-start = ((bf16[16,128,128]{2,1,0:T(8,128)(2,1)}), bf16[16,128,128]{2,1,0:T(8,128)(2,1)S(1)}, u32[]{:S(2)}, u32[]{:S(2)}) async-start(bf16[16,128,128]{2,1,0:T(8,128)(2,1)} %fusion.26), calls=%async_computation | async-start | bytes 1048576 | tf_op jit(solution)/shard_map/all_to_all | solution.py:56
  29.2 4.0 %fusion.152 = (bf16[1,512,2048]{2,1,0:T(8,128)(2,1)}, bf16[1,512,2048]{2,1,0:T(8,128)(2,1)S(1)}) fusion(bf16[2,512,2048]{2,1,0:T(8,128)(2,1)} %param.25), kind=kLoop, calls=%fused_computation.180 | loop fusion | bytes 8388608 | tf_op jit(solution)/shard_map/slice | solution.py:83
  33.2 3.9 %copy.51 = bf16[1,512,2048]{1,2,0:T(8,128)(2,1)} copy(bf16[1,512,2048]{2,1,0:T(8,128)(2,1)} %get-tuple-element.5) | data formatting | bytes 4194304
  37.2 7.2 %all-to-all-done = bf16[16,128,128]{2,1,0:T(8,128)(2,1)S(1)} async-done(((bf16[16,128,128]{2,1,0:T(8,128)(2,1)}), bf16[16,128,128]{2,1,0:T(8,128)(2,1)S(1)}, u32[]{:S(2)}, u32[]{:S(2)}) %all-to-all-start) | async-done | bytes 524320 | tf_op jit(solution)/shard_map/all_to_all | solution.py:56
  45.3 16.0 %all_gather.12 = bf16[128,2048]{1,0:T(8,128)(2,1)S(1)} all-gather(bf16[128,128]{1,0:T(8,128)(2,1)S(1)} %add_convert_fusion.3), channel_id=1, replica_groups=mesh['dp'=4,'tp'=16] {'tp'}, dimensions={1}, use_global_device_ids=true | all-gather | bytes 557056 | tf_op jit(solution)/shard_map/all_gather | solution.py:60
  61.6 2.1 %fusion.18 = f32[128,512]{1,0:T(8,128)S(1)} fusion(bf16[2,2048,512]{2,1,0:T(8,128)(2,1)} %param.23, f32[2048]{0:T(1024)S(1)} %bitcast.154, f32[128]{0:T(128)S(1)} %add_rsqrt_fusion.2, bf16[128,2048]{1,0:T(8,128)(2,1)S(1)} %all_gather.12), kind=kOutput, calls=%fused_computation.18 | convolution fusion | flops 269484032 | bytes 2892288 | tf_op jit(solution)/shard_map/dot_general | solution.py:80
  63.6 4.2 %fusion.24 = bf16[16,128,128]{2,1,0:T(8,128)(2,1)} fusion(bf16[512,16,128]{0,2,1:T(8,128)(2,1)} %bitcast.138, bf16[2,2048,512]{2,1,0:T(8,128)(2,1)} %param.24, f32[128,512]{1,0:T(8,128)S(1)} %fusion.18, f32[2048]{0:T(1024)S(1)} %bitcast.155, f32[128]{0:T(128)S(1)} %add_rsqrt_fusion.2, bf16[128,2048]{1,0:T(8,128)(2,1)S(1)} %all_gather.12), kind=kOutput, calls=%fused_computation.28 | convolution fusion | flops 538574848 | bytes 5513728 | tf_op jit(solution)/shard_map/bk,ktn->tbn/dot_general | solution.py:55
  67.9 5.9 %all-to-all-start.1 = ((bf16[16,128,128]{2,1,0:T(8,128)(2,1)}), bf16[16,128,128]{2,1,0:T(8,128)(2,1)S(1)}, u32[]{:S(2)}, u32[]{:S(2)}) async-start(bf16[16,128,128]{2,1,0:T(8,128)(2,1)} %fusion.24), calls=%async_computation.1 | async-start | bytes 1048576 | tf_op jit(solution)/shard_map/all_to_all | solution.py:56
  76.9 13.1 %all-to-all-done.1 = bf16[16,128,128]{2,1,0:T(8,128)(2,1)S(1)} async-done(((bf16[16,128,128]{2,1,0:T(8,128)(2,1)}), bf16[16,128,128]{2,1,0:T(8,128)(2,1)S(1)}, u32[]{:S(2)}, u32[]{:S(2)}) %all-to-all-start.1) | async-done | bytes 524320 | tf_op jit(solution)/shard_map/all_to_all | solution.py:56
  90.9 16.0 %all_gather.13 = bf16[128,2048]{1,0:T(8,128)(2,1)S(1)} all-gather(bf16[128,128]{1,0:T(8,128)(2,1)S(1)} %add_convert_fusion.2), channel_id=1, replica_groups=mesh['dp'=4,'tp'=16] {'tp'}, dimensions={1}, use_global_device_ids=true | all-gather | bytes 557056 | tf_op jit(solution)/shard_map/all_gather | solution.py:60
  110.4 4.5 %fusion.2 = f32[128,1,128]{2,1,0:T(1,128)S(1)} fusion(bf16[128,128,1]{1,2,0:T(2,128)(2,1)S(1)} %copy.39, bf16[2,128,128,1,128]{4,2,3,1,0:T(8,128)(2,1)} %param.15), kind=kOutput, calls=%fused_computation.2 | convolution fusion | flops 4194304 | bytes 4292608 | tf_op jit(solution)/shard_map/bkgd,bskd->bkgs/dot_general | solution.py:33
  115.4 3.4 %fusion = f32[128,1,128]{2,1,0:T(1,128)S(1)} fusion(bf16[2,128,128,1,128]{4,2,3,1,0:T(8,128)(2,1)} %param.16, bf16[128,128,1]{1,0,2:T(8,128)(2,1)S(1)} %get-tuple-element.10), kind=kOutput, calls=%fused_computation | convolution fusion | flops 4194304 | bytes 4292608 | tf_op jit(solution)/shard_map/bkgs,bskd->bkgd/dot_general | solution.py:41
  118.8 2.4 %fusion.27 = bf16[16,128,128]{2,1,0:T(8,128)(2,1)} fusion(bf16[128,16,128]{0,2,1:T(8,128)(2,1)S(1)} %bitcast.144, f32[128,128]{1,0:T(8,128)S(1)} %bitcast.156, bf16[2,2048,128]{2,1,0:T(8,128)(2,1)} %param.21, f32[128]{0:T(128)S(1)} %get-tuple-element.26, f32[128]{0:T(128)S(1)} %get-tuple-element.25, f32[2048]{0:T(1024)S(1)} %bitcast.148, ...), kind=kOutput, calls=%fused_computation.31 | convolution fusion | flops 135626752 | bytes 2172416 | tf_op jit(solution)/shard_map/bk,ktn->tbn/dot_general | solution.py:55
  121.2 5.9 %all-to-all-start.2 = ((bf16[16,128,128]{2,1,0:T(8,128)(2,1)}), bf16[16,128,128]{2,1,0:T(8,128)(2,1)S(1)}, u32[]{:S(2)}, u32[]{:S(2)}) async-start(bf16[16,128,128]{2,1,0:T(8,128)(2,1)} %fusion.27), calls=%async_computation.2 | async-start | bytes 1048576 | tf_op jit(solution)/shard_map/all_to_all | solution.py:56
  127.1 2.5 %copy.53 = bf16[1,512,2048]{1,2,0:T(8,128)(2,1)} copy(bf16[1,512,2048]{2,1,0:T(8,128)(2,1)S(1)} %get-tuple-element.6) | data formatting | bytes 4194304
  130.7 12.6 %all-to-all-done.2 = bf16[16,128,128]{2,1,0:T(8,128)(2,1)S(1)} async-done(((bf16[16,128,128]{2,1,0:T(8,128)(2,1)}), bf16[16,128,128]{2,1,0:T(8,128)(2,1)S(1)}, u32[]{:S(2)}, u32[]{:S(2)}) %all-to-all-start.2) | async-done | bytes 524320 | tf_op jit(solution)/shard_map/all_to_all | solution.py:56
  144.2 16.1 %all_gather.14 = bf16[128,2048]{1,0:T(8,128)(2,1)S(1)} all-gather(bf16[128,128]{1,0:T(8,128)(2,1)S(1)} %add_convert_fusion.1), channel_id=1, replica_groups=mesh['dp'=4,'tp'=16] {'tp'}, dimensions={1}, use_global_device_ids=true | all-gather | bytes 557056 | tf_op jit(solution)/shard_map/all_gather | solution.py:60
  162.6 3.6 %fusion.25 = bf16[16,128,128]{2,1,0:T(8,128)(2,1)} fusion(bf16[512,16,128]{0,2,1:T(8,128)(2,1)S(1)} %bitcast.139, bf16[2,2048,512]{2,1,0:T(8,128)(2,1)} %param.24, f32[128,512]{1,0:T(8,128)S(1)} %fusion.14, f32[2048]{0:T(1024)S(1)} %bitcast.150, f32[128]{0:T(128)S(1)} %add_rsqrt_fusion, bf16[128,2048]{1,0:T(8,128)(2,1)S(1)} %all_gather.14), kind=kOutput, calls=%fused_computation.29 | convolution fusion | flops 538574848 | bytes 5513728 | tf_op jit(solution)/shard_map/bk,ktn->tbn/dot_general | solution.py:55
  166.2 6.2 %all-to-all-start.3 = ((bf16[16,128,128]{2,1,0:T(8,128)(2,1)}), bf16[16,128,128]{2,1,0:T(8,128)(2,1)S(1)}, u32[]{:S(2)}, u32[]{:S(2)}) async-start(bf16[16,128,128]{2,1,0:T(8,128)(2,1)} %fusion.25), calls=%async_computation.3 | async-start | bytes 1048576 | tf_op jit(solution)/shard_map/all_to_all | solution.py:56
  172.5 16.1 %all-to-all-done.3 = bf16[16,128,128]{2,1,0:T(8,128)(2,1)S(1)} async-done(((bf16[16,128,128]{2,1,0:T(8,128)(2,1)}), bf16[16,128,128]{2,1,0:T(8,128)(2,1)S(1)}, u32[]{:S(2)}, u32[]{:S(2)}) %all-to-all-start.3) | async-done | bytes 524320 | tf_op jit(solution)/shard_map/all_to_all | solution.py:56
  188.8 16.0 %all_gather.15 = bf16[128,2048]{1,0:T(8,128)(2,1)S(1)} all-gather(bf16[128,128]{1,0:T(8,128)(2,1)S(1)} %add_convert_fusion), channel_id=1, replica_groups=mesh['dp'=4,'tp'=16] {'tp'}, dimensions={1}, use_global_device_ids=true | all-gather | bytes 557056 | tf_op jit(solution)/shard_map/all_gather | solution.py:60
  (63 shorter events, 22.7 us)
Async XLA Ops:
  0.0 6.8 %copy-start = (bf16[128,2048]{1,0:T(8,128)(2,1)S(1)}, bf16[128,2048]{1,0:T(8,128)(2,1)}, u32[]{:S(2)}) copy-start(bf16[128,2048]{1,0:T(8,128)(2,1)} %param.13) | copy-start | bytes 1572868
  0.0 6.8 %copy-start.5 = (bf16[2,2048,128]{2,1,0:T(8,128)(2,1)S(1)}, bf16[2,2048,128]{2,1,0:T(8,128)(2,1)}, u32[]{:S(2)}) copy-start(bf16[2,2048,128]{2,1,0:T(8,128)(2,1)} %param.19) | copy-start | bytes 3145732
  3.3 8.9 %copy-start.4 = (s32[128]{0:T(128)S(1)}, s32[128]{0:T(128)}, u32[]{:S(2)}) copy-start(s32[128]{0:T(128)} %param.14) | copy-start | bytes 1540
  7.6 8.4 %copy-start.6 = (bf16[2,2048,128]{2,1,0:T(8,128)(2,1)S(1)}, bf16[2,2048,128]{2,1,0:T(8,128)(2,1)}, u32[]{:S(2)}) copy-start(bf16[2,2048,128]{2,1,0:T(8,128)(2,1)} %param.21) | copy-start | bytes 3145732
  17.4 27.0 %all-to-all-start = ((bf16[16,128,128]{2,1,0:T(8,128)(2,1)}), bf16[16,128,128]{2,1,0:T(8,128)(2,1)S(1)}, u32[]{:S(2)}, u32[]{:S(2)}) async-start(bf16[16,128,128]{2,1,0:T(8,128)(2,1)} %fusion.26), calls=%async_computation | async-start | bytes 1048576 | tf_op jit(solution)/shard_map/all_to_all | solution.py:56
  33.2 4.0 %copy-start.3 = (f32[2,2048]{1,0:T(2,128)S(1)}, f32[2,2048]{1,0:T(2,128)}, u32[]{:S(2)}) copy-start(f32[2,2048]{1,0:T(2,128)} %param.18) | copy-start | bytes 49156
  67.9 22.1 %all-to-all-start.1 = ((bf16[16,128,128]{2,1,0:T(8,128)(2,1)}), bf16[16,128,128]{2,1,0:T(8,128)(2,1)S(1)}, u32[]{:S(2)}, u32[]{:S(2)}) async-start(bf16[16,128,128]{2,1,0:T(8,128)(2,1)} %fusion.24), calls=%async_computation.1 | async-start | bytes 1048576 | tf_op jit(solution)/shard_map/all_to_all | solution.py:56
  110.4 8.3 %copy-start.2 = (bf16[1,128,2048]{1,2,0:T(8,128)(2,1)S(1)}, bf16[1,128,2048]{1,2,0:T(8,128)(2,1)}, u32[]{:S(2)}) copy-start(bf16[1,128,2048]{1,2,0:T(8,128)(2,1)} %copy.52) | copy-start | bytes 1572868
  121.2 22.1 %all-to-all-start.2 = ((bf16[16,128,128]{2,1,0:T(8,128)(2,1)}), bf16[16,128,128]{2,1,0:T(8,128)(2,1)S(1)}, u32[]{:S(2)}, u32[]{:S(2)}) async-start(bf16[16,128,128]{2,1,0:T(8,128)(2,1)} %fusion.27), calls=%async_computation.2 | async-start | bytes 1048576 | tf_op jit(solution)/shard_map/all_to_all | solution.py:56
  130.7 31.9 %copy-start.1 = (bf16[1,512,2048]{1,2,0:T(8,128)(2,1)S(1)}, bf16[1,512,2048]{1,2,0:T(8,128)(2,1)}, u32[]{:S(2)}) copy-start(bf16[1,512,2048]{1,2,0:T(8,128)(2,1)} %copy.53) | copy-start | bytes 6291460
  166.2 22.5 %all-to-all-start.3 = ((bf16[16,128,128]{2,1,0:T(8,128)(2,1)}), bf16[16,128,128]{2,1,0:T(8,128)(2,1)S(1)}, u32[]{:S(2)}, u32[]{:S(2)}) async-start(bf16[16,128,128]{2,1,0:T(8,128)(2,1)} %fusion.25), calls=%async_computation.3 | async-start | bytes 1048576 | tf_op jit(solution)/shard_map/all_to_all | solution.py:56
where the time goes:
time: 207 us; the launch traced here: 206 us
  blocking collectives  64.2 us (31%)
  waiting for transfers between devices  49.1 us (24%)
  matrix products  36.5 us (18%)
  starting transfers between devices  28.7 us (14%)
  local copies, waits for them, and re-layouts  16.9 us (8%)
  other arithmetic  10.1 us (5%)
    all_gather x4, blocking collectives, reduce_add(): return lax.all_gather(new_cols, 'tp', axis=1, tiled=True)  64.2 us
    all_to_all x4, waiting for transfers between devices, reduce_add(): received = lax.all_to_all(partials, 'tp', 0, 0, tiled=True)  49.1 us
    all_to_all x4, starting transfers between devices, reduce_add(): received = lax.all_to_all(partials, 'tp', 0, 0, tiled=True)  28.7 us
    dot_general x4, matrix products, reduce_add(): jnp.einsum('bk,ktn->tbn', activations, weight_blocks, preferred_element_t...  11.7 us
    unnamed x19, local copies, waits for them, and re-layouts  9.63 us
    dot_general x2, matrix products, attention(): jnp.einsum('bkgd,bskd->bkgs', q_group, k_layer, preferred_element_type=jn...  9 us
    dot_general x2, matrix products, attention(): jnp.einsum('bkgs,bskd->bkgd', prob_cache.astype(jnp.bfloat16), v_layer, p...  6.75 us
    dot_general x2, matrix products, local_layers(): jnp.dot(normed_mlp, w_gate[layer_idx], preferred_element_type=jnp.float32)  4.17 us
  transfers between devices with their start and end apart: 4, of which 4 were waited for; matrix products, arithmetic and copies ran while one was open for 8% of the time, Pallas kernels for 0%

commit v1 on v0

v1 whole, which is shorter than its diff:
```python
import functools

import jax
import jax.numpy as jnp
import numpy as np
from jax import lax
from jax.experimental import pallas as pl
from jax.experimental.pallas import tpu as pltpu
from jax.sharding import PartitionSpec as P

NORM_EPS = 1e-5
ROPE_BASE = 10000.0
MESH = pl.DeviceIdType.MESH
F32 = jnp.float32
BF16 = jnp.bfloat16


def nt_dot(a, b):
    return lax.dot_general(a, b, (((1,), (1,)), ((), ())), preferred_element_type=F32)


def dot(a, b):
    return jnp.dot(a, b, preferred_element_type=F32)


def kernel(n, x_ref, len_ref, freq_ref, k_ref, v_ref, an_ref, mn_ref, wq_ref, wk_ref, wv_ref, wo_ref, wg_ref, wu_ref, wd_ref,
           out_ref, hid, act, kbuf, vbuf, wqkv, wo, wg, wu, wd, gains, lens, freqs, cosb, sinb, scores, qb, obuf, ubuf, part, recv, own,
           in_sem, x_sem, w_sem, out_sem, a_send, a_recv, g_send, g_recv):
    chips, toks, width = hid.shape
    half = toks // 2
    layers = kbuf.shape[0]
    head = kbuf.shape[-1]
    seq = kbuf.shape[2]
    me = lax.axis_index("tp")
    z, core = me // 2, lax.rem(me, 2)

    def cp(src, dst, sem):
        return pltpu.make_async_copy(src, dst, sem)

    x_copies = [cp(x_ref.at[:, pl.ds(width * t, width)], hid.at[t], x_sem.at[t]) for t in range(chips)]
    small = [cp(len_ref, lens, in_sem.at[0]), cp(freq_ref, freqs, in_sem.at[1]), cp(an_ref, gains.at[0], in_sem.at[2]),
             cp(mn_ref, gains.at[1], in_sem.at[3])]

    def layer_copies(l):
        return [
            cp(wq_ref.at[l], wqkv.at[l, :, pl.ds(0, head)], w_sem.at[l, 0]),
            cp(wk_ref.at[l], wqkv.at[l, :, pl.ds(head, head)], w_sem.at[l, 1]),
            cp(wv_ref.at[l], wqkv.at[l, :, pl.ds(2 * head, head)], w_sem.at[l, 2]),
            cp(k_ref.at[l], kbuf.at[l], w_sem.at[l, 3]),
            cp(v_ref.at[l], vbuf.at[l], w_sem.at[l, 4]),
            cp(wo_ref.at[l], wo.at[l], w_sem.at[l, 5]),
            cp(wg_ref.at[l], wg.at[l], w_sem.at[l, 6]),
            cp(wu_ref.at[l], wu.at[l], w_sem.at[l, 7]),
            cp(wd_ref.at[l], wd.at[l], w_sem.at[l, 8]),
        ]

    for c in x_copies + small:
        c.start()
    for l in range(layers):
        for c in layer_copies(l):
            c.start()

    barrier = pltpu.get_barrier_semaphore()
    for d in range(1, n):
        pl.semaphore_signal(barrier, inc=1, device_id={"tp": lax.rem(me + d, n)}, device_id_type=MESH)

    for c in small:
        c.wait()
    lens_rows = jnp.transpose(jnp.broadcast_to(lens[...].astype(F32), (toks, toks)))
    angle = lens_rows[:, :head] * freqs[...]
    lane = lax.broadcasted_iota(jnp.int32, (toks, head), 1)
    cosb[...] = jnp.cos(angle)
    sinb[...] = jnp.where(lane < head // 2, -1.0, 1.0) * jnp.sin(angle)
    for c in x_copies:
        c.wait()
    own[...] = hid[z, pl.ds(pl.multiple_of(half * core, half), half), :]
    pl.semaphore_wait(barrier, n - 1)

    def norm(which, l):
        total = jnp.zeros((toks, width), F32)
        for t in range(chips):
            h = hid[t].astype(F32)
            total = total + h * h
        inv = lax.rsqrt(jnp.sum(total, axis=1, keepdims=True) / (chips * width) + NORM_EPS)
        for t in range(chips):
            gain = gains[which, pl.ds(l, 1), pl.ds(width * t, width)]
            act[:, pl.ds(width * t, width)] = (hid[t].astype(F32) * inv * gain).astype(BF16)

    def reduce_gather(src_ref, w_ref, l):
        def chip_block(i, _):
            t = lax.rem(z + 4 + i, chips)
            cols = pl.ds(pl.multiple_of(t * width, width), width)
            part[t] = dot(src_ref[...], w_ref[l, :, cols]).astype(BF16)
            return 0

        lax.fori_loop(0, chips, chip_block, 0)

        def exchange(d):
            to = lax.rem(me + d, n)
            rows = pl.ds(pl.multiple_of(half * lax.rem(to, 2), half), half)
            return pltpu.make_async_remote_copy(
                src_ref=part.at[to // 2, rows], dst_ref=recv.at[d - 1], send_sem=a_send.at[d - 1], recv_sem=a_recv.at[d - 1],
                device_id={"tp": to}, device_id_type=MESH)

        for d in range(1, n):
            exchange(d).start()
        mine = pl.ds(pl.multiple_of(half * core, half), half)
        total = part[z, mine, :].astype(F32)
        for d in range(1, n):
            exchange(d).wait()
            total = total + recv[d - 1].astype(F32)
        own[...] = (own[...].astype(F32) + total).astype(BF16)
        hid[z, mine, :] = own[...]

        def gather(d):
            to = lax.rem(me + d, n)
            return pltpu.make_async_remote_copy(
                src_ref=own, dst_ref=hid.at[z, mine], send_sem=g_send.at[d - 1], recv_sem=g_recv.at[d - 1],
                device_id={"tp": to}, device_id_type=MESH)

        for d in range(1, n):
            gather(d).start()
        for d in range(1, n):
            gather(d).wait()

    def layer(l, _):
        norm(0, l)
        copies = layer_copies(l)
        for c in copies[:3]:
            c.wait()
        qkv = dot(act[...], wqkv[l])
        cos, sin = cosb[...], sinb[...]

        def rope(p):
            return (p * cos + pltpu.roll(p, head // 2, 1) * sin).astype(BF16)

        q = rope(qkv[:, :head])
        k_new = rope(qkv[:, head:2 * head])
        v_new = qkv[:, 2 * head:].astype(BF16)
        scale = head ** -0.5
        logit_new = jnp.sum(q.astype(F32) * k_new.astype(F32), axis=1, keepdims=True) * scale
        qb[...] = q
        copies[3].wait()
        step = 16
        row = lax.broadcasted_iota(jnp.int32, (step, seq), 0)

        def qk(i, _):
            rows = pl.ds(pl.multiple_of(i * step, step), step)
            full = nt_dot(qb[rows, :], kbuf[l, rows].reshape(step * seq, head))
            picked = full[:, :seq]
            for j in range(1, step):
                picked = jnp.where(row == j, full[:, j * seq:(j + 1) * seq], picked)
            scores[rows, :] = picked
            return 0

        lax.fori_loop(0, toks // step, qk, 0)
        lens_rows = jnp.transpose(jnp.broadcast_to(lens[...], (toks, toks)))
        lane = lax.broadcasted_iota(jnp.int32, (toks, seq), 1)
        logits = jnp.where(lane < lens_rows, scores[...] * scale, -1e30)
        top = jnp.maximum(jnp.max(logits, axis=1, keepdims=True), logit_new)
        p = jnp.exp(logits - top)
        p_new = jnp.exp(logit_new - top)
        denom = jnp.sum(p, axis=1, keepdims=True) + p_new
        scores[...] = p
        copies[4].wait()

        def pv(i, _):
            rows = pl.ds(pl.multiple_of(i * step, step), step)
            mine = scores[rows, :]
            spread = jnp.concatenate([jnp.where(row == j, mine, 0.0).astype(BF16) for j in range(step)], axis=1)
            scores[rows, :] = dot(spread, vbuf[l, rows].reshape(step * seq, head))
            return 0

        lax.fori_loop(0, toks // step, pv, 0)
        weighted = scores[...] + p_new.astype(BF16).astype(F32) * v_new.astype(F32)
        obuf[...] = (weighted / denom).astype(BF16)
        copies[5].wait()
        reduce_gather(obuf, wo, l)
        norm(1, l)
        copies[6].wait()
        copies[7].wait()
        for t in range(wg.shape[-1] // 256):
            cols = pl.ds(256 * t, 256)
            gate = dot(act[...], wg[l, :, cols])
            up = dot(act[...], wu[l, :, cols])
            ubuf[:, cols] = (jax.nn.silu(gate) * up).astype(BF16)
        copies[8].wait()
        reduce_gather(ubuf, wd, l)
        return 0

    lax.fori_loop(0, layers, layer, 0)
    outs = [cp(hid.at[t], out_ref.at[:, pl.ds(width * t, width)], out_sem.at[t]) for t in range(chips)]
    for c in outs:
        c.start()
    for c in outs:
        c.wait()


def solution(mesh):
    n = mesh.shape["tp"]
    cache_spec = P(None, "dp", None, "tp", None)
    col_spec = P(None, None, "tp")
    row_spec = P(None, "tp", None)
    in_specs = (P("dp", None), P("dp"), cache_spec, cache_spec, P(), P(), col_spec, col_spec, col_spec, row_spec, col_spec, col_spec, row_spec)

    def step(x, lengths, k_cache, v_cache, attn_norm, mlp_norm, w_q, w_k, w_v, w_o, w_gate, w_up, w_down):
        toks, dim = x.shape
        layers, _, seq, _, head = k_cache.shape
        ff = w_gate.shape[2]
        chips = n // 2
        width = dim // chips
        half = toks // 2
        k = k_cache.reshape(layers, toks, seq, head)
        v = v_cache.reshape(layers, toks, seq, head)
        freq = ROPE_BASE ** (-np.arange(0, head, 2, dtype=np.float32) / head)
        freq = jnp.asarray(np.concatenate([freq, freq])[None, :].astype(np.float32))
        dma = pltpu.SemaphoreType.DMA
        scratch = [
            pltpu.VMEM((chips, toks, width), BF16),
            pltpu.VMEM((toks, dim), BF16),
            pltpu.VMEM((layers, toks, seq, head), BF16),
            pltpu.VMEM((layers, toks, seq, head), BF16),
            pltpu.VMEM((layers, dim, 3 * head), BF16),
            pltpu.VMEM((layers, head, dim), BF16),
            pltpu.VMEM((layers, dim, ff), BF16),
            pltpu.VMEM((layers, dim, ff), BF16),
            pltpu.VMEM((layers, ff, dim), BF16),
            pltpu.VMEM((2, layers, dim), F32),
            pltpu.VMEM((1, toks), jnp.int32),
            pltpu.VMEM((1, head), F32),
            pltpu.VMEM((toks, head), F32),
            pltpu.VMEM((toks, head), F32),
            pltpu.VMEM((toks, seq), F32),
            pltpu.VMEM((toks, head), BF16),
            pltpu.VMEM((toks, head), BF16),
            pltpu.VMEM((toks, ff), BF16),
            pltpu.VMEM((chips, toks, width), BF16),
            pltpu.VMEM((n - 1, half, width), BF16),
            pltpu.VMEM((half, width), BF16),
            dma((4,)), dma((chips,)), dma((layers, 9)), dma((chips,)),
            dma((n - 1,)), dma((n - 1,)), dma((n - 1,)), dma((n - 1,)),
        ]
        anyspace = pl.BlockSpec(memory_space=pl.ANY)
        return pl.pallas_call(
            functools.partial(kernel, n),
            out_shape=jax.ShapeDtypeStruct((toks, dim), BF16),
            in_specs=[anyspace] * 14,
            out_specs=anyspace,
            scratch_shapes=scratch,
            compiler_params=pltpu.CompilerParams(collective_id=0, has_side_effects=True, vmem_limit_bytes=60 * 1024 * 1024),
        )(x, lengths.reshape(1, toks), freq, k, v, attn_norm, mlp_norm, w_q, w_k, w_v, w_o, w_gate, w_up, w_down)

    return jax.shard_map(step, mesh=mesh, in_specs=in_specs, out_specs=P("dp", None), check_vma=False)
```

time: 207 us -> 152 us (0.73)
  Pallas kernels: 0 us -> 150 us
  blocking collectives: 64.2 us -> 0 us
  waiting for transfers between devices: 49.1 us -> 0 us
  matrix products: 36.5 us -> 0 us
  starting transfers between devices: 28.7 us -> 0 us
  local copies, waits for them, and re-layouts: 16.9 us -> 1.88 us
  other arithmetic: 10.1 us -> 0 us
    pallas_call x0 -> x1, Pallas kernels: none -> 150 us  [step(): pl.pallas_call(functools.partial(kernel, n), out_shape=jax.ShapeDtypeStru...]
    all_gather x4 -> x0, blocking collectives: 64.2 us -> none  [reduce_add(): return lax.all_gather(new_cols, 'tp', axis=1, tiled=True)]
    all_to_all x4 -> x0, waiting for transfers between devices: 49.1 us -> none  [reduce_add(): received = lax.all_to_all(partials, 'tp', 0, 0, tiled=True)]
    dot_general x14 -> x0, matrix products: 36.5 us -> none  [the longest x4 11.7 us: reduce_add(): jnp.einsum('bk,ktn->tbn', activations, weight_blocks, preferred_element_t...]
    all_to_all x4 -> x0, starting transfers between devices: 28.7 us -> none  [reduce_add(): received = lax.all_to_all(partials, 'tp', 0, 0, tiled=True)]
    unnamed x19 -> x1, local copies, waits for them, and re-layouts: 9.63 us -> 1.88 us
    slice x4 -> x0, local copies, waits for them, and re-layouts: 6.99 us -> none  [the longest x1 3.97 us: local_layers(): residual = reduce_add(mlp_act, w_down[layer_idx], hidden_f)]
    convert_element_type x11 -> x0, other arithmetic: 6.63 us -> none  [the longest x4 2.6 us: reduce_add(): (own_cols + jnp.sum(received.astype(jnp.float32), axis=0)).astype(jnp.bfl...]
  transfers between devices with their start and end apart: 4 -> 0, of which waited for: 4 -> 0; matrix products, arithmetic and copies ran while one was open for 8% -> 0% of each run, Pallas kernels for 0% -> 0%
where the time goes in v1:
time: 152 us
  Pallas kernels  150 us (99%)
  local copies, waits for them, and re-layouts  1.88 us (1%)
    pallas_call x1, Pallas kernels, step(): pl.pallas_call(functools.partial(kernel, n), out_shape=jax.ShapeDtypeStru...  150 us

profile of v1, /device:TPU:21, one launch (start us, length us, event | category | flops | bytes accessed | tf_op | source)
XLA Modules:
  0.0 152.1 jit_solution(11516836347953070496)
XLA Ops:
  0.0 150.3 %shard_map.136 = bf16[128,2048]{1,0:T(8,128)(2,1)} custom-call(bf16[128,2048]{1,0:T(8,128)(2,1)} %x_ref.1, s32[1,128]{1,0:T(1,128)} %bitcast.5, f32[1,128]{1,0:T(1,128)} %constant.2.clone.freq_ref, bf16[2,128,128,128]{3,2,1,0:T(8,128)(2,1)} %bitcast.3, bf16[2,128,128,128]{3,2,1,0:T(8,128)(2,1)} %bitcast.4, f32[2,2048]{1,0:T(2,128)} %an_ref.1, ...), custom_call_target="tpu_custom_call" | custom-call | tf_op jit(solution)/shard_map/pallas_call | solution.py:244
  150.3 1.9 %copy.16 = bf16[128,2048]{1,0:T(8,128)(2,1)} copy(bf16[128,2048]{1,0:T(8,128)(2,1)} %shard_map.136) | data formatting | bytes 1048576
